TPU v7x, 32 devices: a whole 2x2x4 slice. The times are simulated.
32 devices in a mesh: gx: 4 (over x, core), gy: 8 (over z, y).
Axes of the slice: x: 2, y: 2, z: 4, core: 2. Of those that a mesh axis runs over, the one named last changes fastest.
Arguments:
- fine_start: float32 [3, 1024, 4096], P(None, 'gx', 'gy'), may hold values from -6 to 6
- fine_known: float32 [3, 1024, 4096], P(None, 'gx', 'gy'), may hold values from -18 to 18
- fine_mu: float32 [1024, 4096], P('gx', 'gy'), may hold values from 1 to 10
- coarse_start: float32 [3, 512, 2048], P(None, ('gx', 'gy')), may hold values from -6 to 6
- coarse_known: float32 [3, 512, 2048], P(None, ('gx', 'gy')), may hold values from -18 to 18
- coarse_mu: float32 [512, 2048], P(('gx', 'gy')), may hold values from 1 to 10
Outputs:
- fine_ghost: float32 [3, 1024, 4096], P(None, 'gx', 'gy')
- coarse_ghost: float32 [3, 512, 2048], P(None, ('gx', 'gy'))
- norms: float32 [3], replicated
All inputs are finite; a program needn't handle non-finite values.
Results may differ from a plain program's by a relative error of at most 0.0001.
Values sent between devices are 32-bit elements; how exact they have to be, the bound alone decides.
A program may use at most 128 MiB of HBM per device.

v0:
```python
import functools

import jax
import jax.numpy as jnp
from jax import lax
from jax.experimental import pallas as pl
from jax.experimental.pallas import tpu as pltpu
from jax.sharding import PartitionSpec as P

ITERS = 3
LANES = 128
SUB = 8
MESH = pl.DeviceIdType.MESH
DIRECTIONS = ((-1, 0), (1, 0), (0, -1), (0, 1), (-1, -1), (1, 1), (-1, 1), (1, -1))


def lane_index():
    return lax.broadcasted_iota(jnp.int32, (SUB, LANES), 1)


def roll_lanes(cells, shift):
    shift = shift % LANES
    return cells if shift == 0 else pltpu.roll(cells, shift, 1)


def from_left(halves, halo):
    first = lane_index() == 0
    rolled = [roll_lanes(cells, 1) for cells in halves]
    return [jnp.where(first, before, own) for before, own in zip([halo] + rolled[:-1], rolled)]


def from_right(halves, halo):
    last = lane_index() == LANES - 1
    rolled = [roll_lanes(cells, LANES - 1) for cells in halves]
    return [jnp.where(last, after, own) for own, after in zip(rolled, rolled[1:] + [halo])]


def kernel(
    n_gx,
    n_gy,
    cells_total,
    fine_start,
    fine_known,
    fine_mu,
    coarse_start,
    coarse_known,
    coarse_mu,
    fine_out,
    coarse_out,
    norms_out,
    raw_start,
    raw_known,
    raw_mu,
    fine,
    known,
    diag,
    inverse,
    patch_start,
    patch_known,
    patch_mu,
    coarse,
    patch_out,
    row_send,
    col_send,
    col_out,
    row_recv,
    col_recv,
    corner_recv,
    left_halo,
    right_halo,
    norm_x,
    norm_y,
    load_sem,
    store_sem,
    own_sem,
    move_send,
    move_recv,
    halo_send,
    halo_recv,
    back_own,
    back_send,
    back_recv,
    normx_send,
    normx_recv,
    normy_send,
    normy_recv,
):
    gx = lax.axis_index("gx")
    gy = lax.axis_index("gy")
    comps, rows, width = patch_start.shape
    halves = width // LANES
    blocks = rows // SUB
    own_rows = coarse_start.shape[1]
    lane = lane_index()

    loads = []
    for which, (source, target) in enumerate(
        ((fine_start, raw_start), (fine_mu, raw_mu), (fine_known, raw_known))
    ):
        for tile in range(2 * halves):
            at = pl.ds(tile * LANES, LANES)
            view = source.at[:, at] if len(source.shape) == 2 else source.at[:, :, at]
            loads.append(
                pltpu.make_async_copy(view, target.at[tile], load_sem.at[which, tile])
            )
    for copy in loads:
        copy.start()

    row_recv[...] = jnp.zeros_like(row_recv)
    col_recv[...] = jnp.zeros_like(col_recv)
    corner_recv[...] = jnp.zeros_like(corner_recv)
    col_send[...] = jnp.zeros_like(col_send)
    row_send[...] = jnp.zeros_like(row_send)

    barrier = pltpu.get_barrier_semaphore()

    def greet_gy(step, carry):
        pl.semaphore_signal(
            barrier, inc=1, device_id={"gy": lax.rem(gy + step, n_gy)}, device_id_type=MESH
        )
        return carry

    def greet_gx(step, carry):
        pl.semaphore_signal(
            barrier, inc=1, device_id={"gx": lax.rem(gx + step, n_gx)}, device_id_type=MESH
        )
        return carry

    lax.fori_loop(1, n_gy, greet_gy, 0)
    lax.fori_loop(1, n_gx, greet_gx, 0)

    def inside(direction):
        dx, dy = DIRECTIONS[direction]
        checks = []
        if dx:
            checks.append(gx > 0 if dx < 0 else gx < n_gx - 1)
        if dy:
            checks.append(gy > 0 if dy < 0 else gy < n_gy - 1)
        return functools.reduce(jnp.logical_and, checks)

    for direction in range(4, 8):
        dx, dy = DIRECTIONS[direction]

        @pl.when(inside(direction))
        def _():
            pl.semaphore_signal(
                barrier, inc=1, device_id={"gx": gx + dx, "gy": gy + dy}, device_id_type=MESH
            )

    sides_x = (gx > 0).astype(jnp.int32) + (gx < n_gx - 1).astype(jnp.int32)
    sides_y = (gy > 0).astype(jnp.int32) + (gy < n_gy - 1).astype(jnp.int32)
    pl.semaphore_wait(barrier, n_gy - 1 + n_gx - 1 + sides_x * sides_y)

    moved = ((coarse_start, patch_start), (coarse_known, patch_known), (coarse_mu, patch_mu))

    def move(which, owner, place, sem):
        source, target = moved[which]
        columns = pl.ds(pl.multiple_of(owner * width, LANES), width)
        lines = pl.ds(pl.multiple_of(place * own_rows, SUB), own_rows)
        if len(source.shape) == 2:
            return source.at[:, columns], target.at[lines, :]
        return source.at[:, :, columns], target.at[:, lines, :]

    def own_move(which):
        source, target = move(which, gy, gy, None)
        return pltpu.make_async_copy(source, target, own_sem.at[which])

    def peer_move(which, step):
        peer = lax.rem(gy + step, n_gy)
        source, target = move(which, peer, gy, None)
        return pltpu.make_async_remote_copy(
            source,
            target,
            move_send.at[which, step],
            move_recv.at[which, step],
            device_id={"gy": peer},
            device_id_type=MESH,
        )

    def wait_moves(which):
        own_move(which).wait()

        def body(step, carry):
            peer = lax.rem(gy + n_gy - step, n_gy)
            source, target = move(which, gy, peer, None)
            pltpu.make_async_remote_copy(
                source,
                target,
                move_send.at[which, step],
                move_recv.at[which, step],
                device_id={"gy": lax.rem(gy + step, n_gy)},
                device_id_type=MESH,
            ).wait()
            return carry

        lax.fori_loop(1, n_gy, body, 0)

    for which in range(3):

        def send_step(step, carry, which=which):
            peer_move(which, step).start()
            return carry

        lax.fori_loop(1, n_gy, send_step, 0)
        own_move(which).start()

    half_lane = lane < LANES // 2
    evens_first = jnp.where(half_lane, 2 * lane, 2 * lane - LANES + 1)
    odds_first = jnp.where(half_lane, 2 * lane + 1, 2 * lane - LANES)

    def split_columns(a, b):
        a = jnp.take_along_axis(a, evens_first, axis=1)
        b = jnp.take_along_axis(b, odds_first, axis=1)
        return (
            jnp.where(half_lane, a, b),
            pltpu.roll(jnp.where(half_lane, b, a), LANES // 2, 1),
        )

    def split_field(raw, put):
        def body(i, carry):
            comp, block = i // blocks, i % blocks
            for parity in range(2):
                for half in range(halves):
                    at = pl.ds(block * 2 * SUB + parity, SUB, stride=2)
                    even, odd = split_columns(
                        raw[2 * half, comp, at, :], raw[2 * half + 1, comp, at, :]
                    )
                    put(comp, parity, 0, half, block, even)
                    put(comp, parity, 1, half, block, odd)
            return carry

        lax.fori_loop(0, comps * blocks, body, 0)

    def rows_of(block, shift=0):
        if shift == 0:
            return pl.ds(pl.multiple_of(block * SUB + SUB, SUB), SUB)
        return pl.ds(block * SUB + SUB + shift, SUB)

    def plain(block):
        return pl.ds(pl.multiple_of(block * SUB, SUB), SUB)

    def put_start(comp, parity, side, half, block, cells):
        fine[0, comp, parity, side, half, rows_of(block), :] = cells

    def put_known(comp, parity, side, half, block, cells):
        known[comp, parity, side, half, plain(block), :] = cells

    def split_mu(block, carry):
        for parity in range(2):
            for half in range(halves):
                at = pl.ds(block * 2 * SUB + parity, SUB, stride=2)
                both = split_columns(raw_mu[2 * half, at, :], raw_mu[2 * half + 1, at, :])
                for side in range(2):
                    total = both[side] + 1.0
                    diag[parity, side, half, plain(block), :] = total
                    inverse[parity, side, half, plain(block), :] = 1.0 / total
        return carry

    tiles = 2 * halves
    for copy in loads[:tiles]:
        copy.wait()
    split_field(raw_start, put_start)
    for copy in loads[tiles : 2 * tiles]:
        copy.wait()
    lax.fori_loop(0, blocks, split_mu, 0)
    for copy in loads[2 * tiles :]:
        copy.wait()
    split_field(raw_known, put_known)

    wait_moves(0)

    def place_start(i, carry):
        comp, block = i // blocks, i % blocks
        for half in range(halves):
            coarse[0, comp, half, rows_of(block), :] = patch_start[
                comp, plain(block), half * LANES : (half + 1) * LANES
            ]
        return carry

    lax.fori_loop(0, comps * blocks, place_start, 0)

    def exchange(sweep, buf):
        for way, (parity, line) in enumerate(((0, SUB), (1, SUB + rows - 1))):
            for half in range(halves):
                for comp in range(comps):
                    for side in range(2):
                        at = 2 * comp + side
                        row_send[sweep, way, half, at : at + 1, :] = fine[
                            buf, comp, parity, side, half, line : line + 1, :
                        ]
                    row_send[sweep, way, half, SUB + comp : SUB + comp + 1, :] = coarse[
                        buf, comp, half, line : line + 1, :
                    ]

        def gather(block, carry):
            for way, (half, at, side) in enumerate(((0, 0, 0), (halves - 1, LANES - 1, 1))):
                cells = jnp.zeros((SUB, LANES), jnp.float32)
                for k in range(3 * comps):
                    if k < 2 * comps:
                        edge = fine[buf, k // 2, k % 2, side, half, rows_of(block), :]
                    else:
                        edge = coarse[buf, k - 2 * comps, half, rows_of(block), :]
                    cells = jnp.where(lane == k, roll_lanes(edge, k - at), cells)
                col_send[way, plain(block), :] = cells
            return carry

        lax.fori_loop(0, blocks, gather, 0)
        for way in range(2):
            turned = col_send[way, :, :].T
            col_turned = turned[: 2 * SUB]
            col_out[sweep, way, :, :] = col_turned

        def message(direction):
            dx, dy = DIRECTIONS[direction]
            way = direction % 2
            if direction < 2:
                source, target = row_send.at[sweep, way], row_recv.at[sweep, 1 - way]
            elif direction < 4:
                source = col_out.at[sweep, way]
                target = col_recv.at[sweep, 1 - way, pl.ds(0, 2 * SUB), :]
            else:
                half = 0 if dy < 0 else halves - 1
                source = row_send.at[sweep, 0 if dx < 0 else 1, half, pl.ds(SUB, SUB), :]
                target = corner_recv.at[sweep, (direction ^ 1) - 4]
            return pltpu.make_async_remote_copy(
                source,
                target,
                halo_send.at[sweep, direction],
                halo_recv.at[sweep, direction ^ 1],
                device_id={"gx": gx + dx, "gy": gy + dy},
                device_id_type=MESH,
            )

        for direction in range(8):

            @pl.when(inside(direction))
            def _():
                message(direction).start()

        for direction in range(8):

            @pl.when(inside(direction))
            def _():
                message(direction).wait_send()
                message(direction ^ 1).wait_recv()

        for half in range(halves):
            for comp in range(comps):
                for side in range(2):
                    at = 2 * comp + side
                    fine[buf, comp, 1, side, half, SUB - 1 : SUB, :] = row_recv[
                        sweep, 0, half, at : at + 1, :
                    ]
                    fine[buf, comp, 0, side, half, SUB + rows : SUB + rows + 1, :] = row_recv[
                        sweep, 1, half, at : at + 1, :
                    ]
                for way, line in enumerate((SUB - 1, SUB + rows)):
                    coarse[buf, comp, half, line : line + 1, :] = row_recv[
                        sweep, way, half, SUB + comp : SUB + comp + 1, :
                    ]
        left_halo[SUB : SUB + rows, :] = col_recv[sweep, 0].T
        right_halo[SUB : SUB + rows, :] = col_recv[sweep, 1].T
        for target, corners, at in ((left_halo, (0, 3), LANES - 1), (right_halo, (2, 1), 0)):
            for corner, line in zip(corners, (SUB - 1, SUB + rows)):
                block = corner_recv[sweep, corner]
                held = jnp.zeros((SUB, LANES), jnp.float32)
                for comp in range(comps):
                    k = 2 * comps + comp
                    held = jnp.where(
                        lane == k, roll_lanes(pltpu.roll(block, (SUB - comp) % SUB, 0)
                                              if comp else block, k - at), held
                    )
                target[line : line + 1, :] = held[0:1, :]

    def halo_pair(k, lines):
        left = pltpu.roll(left_halo[lines, :], lax.rem(LANES - k, LANES), 1)
        right = pltpu.roll(right_halo[lines, :], lax.rem(LANES - 1 - k, LANES), 1)
        return left, right

    def coarse_pass(buf, last):
        def body(i, total):
            comp, block = i // blocks, i % blocks
            k = 2 * comps + comp
            left, right = halo_pair(k, rows_of(block))
            own = [coarse[buf, comp, half, rows_of(block), :] for half in range(halves)]
            lefts, rights = from_left(own, left), from_right(own, right)
            for half in range(halves):
                columns = slice(half * LANES, (half + 1) * LANES)
                near = (
                    coarse[buf, comp, half, rows_of(block, 1), :]
                    + coarse[buf, comp, half, rows_of(block, -1), :]
                    + rights[half]
                    + lefts[half]
                )
                below = (
                    fine[buf, comp, 0, 0, half, rows_of(block), :]
                    + fine[buf, comp, 1, 0, half, rows_of(block), :]
                    + fine[buf, comp, 0, 1, half, rows_of(block), :]
                    + fine[buf, comp, 1, 1, half, rows_of(block), :]
                )
                scale = patch_mu[plain(block), columns] + 1.0
                res = (
                    patch_known[comp, plain(block), columns]
                    + 0.25 * near
                    + 0.125 * below
                    - scale * own[half]
                )
                total = total + res * res
                new = own[half] + res / scale
                if last:
                    patch_out[comp, plain(block), columns] = new
                else:
                    coarse[1 - buf, comp, half, rows_of(block), :] = new
            return total

        return lax.fori_loop(0, comps * blocks, body, jnp.zeros((SUB, LANES), jnp.float32))

    def fine_pass(buf):
        def body(i, total):
            comp, block = i // blocks, i % blocks
            k = 2 * comps + comp
            mid = [coarse[buf, comp, half, rows_of(block), :] for half in range(halves)]
            mid_left, mid_right = halo_pair(k, rows_of(block))
            for parity in range(2):
                shift = 1 if parity else -1
                far_left, far_right = halo_pair(k, rows_of(block, shift))
                line = [
                    0.75 * mid[half]
                    + 0.25 * coarse[buf, comp, half, rows_of(block, shift), :]
                    for half in range(halves)
                ]
                line_left = from_left(line, 0.75 * mid_left + 0.25 * far_left)
                line_right = from_right(line, 0.75 * mid_right + 0.25 * far_right)
                fine_left, fine_right = halo_pair(2 * comp + parity, rows_of(block))
                evens = [fine[buf, comp, parity, 0, half, rows_of(block), :] for half in range(halves)]
                odds = [fine[buf, comp, parity, 1, half, rows_of(block), :] for half in range(halves)]
                before, after = from_left(odds, fine_left), from_right(evens, fine_right)
                for half in range(halves):
                    for side in range(2):
                        own = odds[half] if side else evens[half]
                        lateral = (
                            evens[half] + after[half] if side else odds[half] + before[half]
                        )
                        near = (
                            fine[buf, comp, 1 - parity, side, half, rows_of(block), :]
                            + fine[buf, comp, 1 - parity, side, half, rows_of(block, shift), :]
                            + lateral
                        )
                        spread = 0.75 * line[half] + 0.25 * (
                            line_right[half] if side else line_left[half]
                        )
                        res = (
                            known[comp, parity, side, half, plain(block), :]
                            + 0.25 * near
                            + 0.5 * spread
                            - diag[parity, side, half, plain(block), :] * own
                        )
                        total = total + res * res
                        fine[1 - buf, comp, parity, side, half, rows_of(block), :] = (
                            own + res * inverse[parity, side, half, plain(block), :]
                        )
            return total

        return lax.fori_loop(0, comps * blocks, body, jnp.zeros((SUB, LANES), jnp.float32))

    def back_place(owner, place):
        return (
            patch_out.at[:, pl.ds(pl.multiple_of(owner * own_rows, SUB), own_rows), :],
            coarse_out.at[:, :, pl.ds(pl.multiple_of(place * width, LANES), width)],
        )

    def back_move(step, place_step):
        peer = lax.rem(gy + step, n_gy)
        source, _ = back_place(peer, gy)
        _, target = back_place(peer, lax.rem(gy + place_step, n_gy))
        return pltpu.make_async_remote_copy(
            source,
            target,
            back_send.at[step],
            back_recv.at[step],
            device_id={"gy": peer},
            device_id_type=MESH,
        )

    def back_start(step, carry):
        back_move(step, 0).start()
        return carry

    def back_wait(step, carry):
        back_move(step, n_gy - step).wait()
        return carry

    own_back = pltpu.make_async_copy(*back_place(gy, gy), back_own.at[0])
    row = lax.broadcasted_iota(jnp.int32, (SUB, LANES), 0)
    sums = jnp.zeros((SUB, LANES), jnp.float32)
    for sweep in range(ITERS):
        buf = sweep % 2
        last = sweep == ITERS - 1
        exchange(sweep, buf)
        if sweep == 0:
            wait_moves(1)
            wait_moves(2)
        total = coarse_pass(buf, last)
        if last:
            lax.fori_loop(1, n_gy, back_start, 0)
            own_back.start()
        total = total + fine_pass(buf)
        sums = jnp.where(row == sweep, jnp.sum(total, axis=0, keepdims=True), sums)

    def spread_sum(slots, axis, me, count, send_sems, recv_sems, between):
        def message(step, place_step):
            peer = lax.rem(me + step, count)
            return pltpu.make_async_remote_copy(
                slots.at[me],
                slots.at[lax.rem(me + place_step, count)],
                send_sems.at[step],
                recv_sems.at[step],
                device_id={axis: peer},
                device_id_type=MESH,
            )

        def start(step, carry):
            message(step, 0).start()
            return carry

        def wait(step, carry):
            message(step, count - step).wait()
            return carry

        lax.fori_loop(1, count, start, 0)
        between()
        lax.fori_loop(1, count, wait, 0)
        return lax.fori_loop(
            0, count, lambda i, acc: acc + slots[i], jnp.zeros((SUB, LANES), jnp.float32)
        )

    final = ITERS % 2
    weave_a = jnp.where(lane % 2 == 0, lane // 2, lane // 2 + LANES // 2)
    weave_b = jnp.where(lane % 2 == 0, lane // 2 + LANES // 2, lane // 2)

    def weave(i, carry):
        comp, block = i // blocks, i % blocks
        for parity in range(2):
            for half in range(halves):
                even = fine[final, comp, parity, 0, half, rows_of(block), :]
                odd = pltpu.roll(fine[final, comp, parity, 1, half, rows_of(block), :], LANES // 2, 1)
                at = pl.ds(block * 2 * SUB + parity, SUB, stride=2)
                raw_start[2 * half, comp, at, :] = jnp.take_along_axis(
                    jnp.where(half_lane, even, odd), weave_a, axis=1
                )
                raw_start[2 * half + 1, comp, at, :] = jnp.take_along_axis(
                    jnp.where(half_lane, odd, even), weave_b, axis=1
                )
        return carry

    stores = [
        pltpu.make_async_copy(
            raw_start.at[tile],
            fine_out.at[:, :, pl.ds(tile * LANES, LANES)],
            store_sem.at[tile],
        )
        for tile in range(tiles)
    ]

    def put_fine():
        lax.fori_loop(0, comps * blocks, weave, 0)
        for copy in stores:
            copy.start()

    norm_x[gx] = sums
    partial = spread_sum(norm_x, "gx", gx, n_gx, normx_send, normx_recv, put_fine)
    norm_y[gy] = partial
    whole = spread_sum(norm_y, "gy", gy, n_gy, normy_send, normy_recv, lambda: None)
    root = jnp.sqrt(jnp.sum(whole, axis=1, keepdims=True) / cells_total)
    norms_out[...] = jnp.broadcast_to(root, norms_out.shape)

    for copy in stores:
        copy.wait()
    own_back.wait()
    lax.fori_loop(1, n_gy, back_wait, 0)


def on_device(n_gx, n_gy, fine_start, fine_known, fine_mu, coarse_start, coarse_known, coarse_mu):
    comps, fine_rows, fine_cols = fine_start.shape
    rows, width = fine_rows // 2, fine_cols // 2
    halves = width // LANES
    tiles = 2 * halves
    padded = rows + 2 * SUB
    cells_total = 3.0 * (fine_mu.size + coarse_mu.size) * n_gx * n_gy
    f32 = jnp.float32
    dma = pltpu.SemaphoreType.DMA
    anywhere = pl.BlockSpec(memory_space=pl.ANY)
    fine_ghost, coarse_ghost, norms = pl.pallas_call(
        functools.partial(kernel, n_gx, n_gy, cells_total),
        out_shape=(
            jax.ShapeDtypeStruct(fine_start.shape, f32),
            jax.ShapeDtypeStruct(coarse_start.shape, f32),
            jax.ShapeDtypeStruct((SUB, LANES), f32),
        ),
        in_specs=[anywhere] * 6,
        out_specs=(anywhere, anywhere, pl.BlockSpec(memory_space=pltpu.VMEM)),
        scratch_shapes=[
            pltpu.VMEM((tiles, comps, fine_rows, LANES), f32),
            pltpu.VMEM((tiles, comps, fine_rows, LANES), f32),
            pltpu.VMEM((tiles, fine_rows, LANES), f32),
            pltpu.VMEM((2, comps, 2, 2, halves, padded, LANES), f32),
            pltpu.VMEM((comps, 2, 2, halves, rows, LANES), f32),
            pltpu.VMEM((2, 2, halves, rows, LANES), f32),
            pltpu.VMEM((2, 2, halves, rows, LANES), f32),
            pltpu.VMEM((comps, rows, width), f32),
            pltpu.VMEM((comps, rows, width), f32),
            pltpu.VMEM((rows, width), f32),
            pltpu.VMEM((2, comps, halves, padded, LANES), f32),
            pltpu.VMEM((comps, rows, width), f32),
            pltpu.VMEM((ITERS, 2, halves, 2 * SUB, LANES), f32),
            pltpu.VMEM((2, rows, LANES), f32),
            pltpu.VMEM((ITERS, 2, 2 * SUB, rows), f32),
            pltpu.VMEM((ITERS, 2, halves, 2 * SUB, LANES), f32),
            pltpu.VMEM((ITERS, 2, LANES, rows), f32),
            pltpu.VMEM((ITERS, 4, SUB, LANES), f32),
            pltpu.VMEM((padded, LANES), f32),
            pltpu.VMEM((padded, LANES), f32),
            pltpu.VMEM((n_gx, SUB, LANES), f32),
            pltpu.VMEM((n_gy, SUB, LANES), f32),
            dma((3, tiles)),
            dma((tiles,)),
            dma((3,)),
            dma((3, n_gy)),
            dma((3, n_gy)),
            dma((ITERS, 8)),
            dma((ITERS, 8)),
            dma((1,)),
            dma((n_gy,)),
            dma((n_gy,)),
            dma((n_gx,)),
            dma((n_gx,)),
            dma((n_gy,)),
            dma((n_gy,)),
        ],
        compiler_params=pltpu.CompilerParams(
            collective_id=0, has_side_effects=True, vmem_limit_bytes=48 * 1024 * 1024
        ),
    )(fine_start, fine_known, fine_mu, coarse_start, coarse_known, coarse_mu)
    return fine_ghost, coarse_ghost, norms[:ITERS, 0]


def solution(mesh):
    n_gx, n_gy = mesh.shape["gx"], mesh.shape["gy"]
    return jax.shard_map(
        functools.partial(on_device, n_gx, n_gy),
        mesh=mesh,
        in_specs=(
            P(None, "gx", "gy"),
            P(None, "gx", "gy"),
            P("gx", "gy"),
            P(None, ("gx", "gy"), None),
            P(None, ("gx", "gy"), None),
            P(("gx", "gy"), None),
        ),
        out_specs=(P(None, "gx", "gy"), P(None, ("gx", "gy"), None), P()),
        check_vma=False,
    )
```

profile of v0, /device:TPU:0, one launch (start us, length us, event | category | flops | bytes accessed | tf_op | source)
XLA Modules:
  0.0 87.5 jit_solution(12529449909139449123)
XLA Ops:
  0.6 0.0 copy-start
  0.6 1.4 %copy-done = f32[3,256,512]{2,1,0:T(8,128)S(1)} copy-done((f32[3,256,512]{2,1,0:T(8,128)S(1)}, f32[3,256,512]{2,1,0:T(8,128)}, u32[]{:S(2)}) %copy-start) | copy-done | bytes 1572888
  2.0 0.0 copy-start.1
  2.0 1.0 %copy-done.1 = f32[256,512]{1,0:T(8,128)S(1)} copy-done((f32[256,512]{1,0:T(8,128)S(1)}, f32[256,512]{1,0:T(8,128)}, u32[]{:S(2)}) %copy-start.1) | copy-done | bytes 524312
  3.1 0.0 copy-start.2
  3.1 1.0 %copy-done.2 = f32[3,16,2048]{2,1,0:T(8,128)S(1)} copy-done((f32[3,16,2048]{2,1,0:T(8,128)S(1)}, f32[3,16,2048]{2,1,0:T(8,128)}, u32[]{:S(2)}) %copy-start.2) | copy-done | bytes 393240
  4.1 0.0 copy-start.3
  4.1 1.0 %copy-done.3 = f32[3,16,2048]{2,1,0:T(8,128)S(1)} copy-done((f32[3,16,2048]{2,1,0:T(8,128)S(1)}, f32[3,16,2048]{2,1,0:T(8,128)}, u32[]{:S(2)}) %copy-start.3) | copy-done | bytes 393240
  5.1 0.0 copy-start.4
  5.1 0.9 %copy-done.4 = f32[16,2048]{1,0:T(8,128)S(1)} copy-done((f32[16,2048]{1,0:T(8,128)S(1)}, f32[16,2048]{1,0:T(8,128)}, u32[]{:S(2)}) %copy-start.4) | copy-done | bytes 131096
  6.0 79.0 %shard_map.85 = (f32[3,256,512]{2,1,0:T(8,128)S(1)}, f32[3,16,2048]{2,1,0:T(8,128)S(1)}, f32[8,128]{1,0:T(8,128)S(1)}) custom-call(f32[3,256,512]{2,1,0:T(8,128)S(1)} %copy-done, f32[3,256,512]{2,1,0:T(8,128)} %fine_known.1, f32[256,512]{1,0:T(8,128)S(1)} %copy-done.1, f32[3,16,2048]{2,1,0:T(8,128)S(1)} %copy-done.2, f32[3,16,2048]{2,1,0:T(8,128)S(1)} %copy-done.3, ...), custom_call_target="tpu_custom_call" | custom-call | tf_op jit(solution)/shard_map/pallas_call | solution.py:593
  85.0 0.6 slice_reduce_fusion
  85.6 1.1 %copy.11 = f32[3,256,512]{2,1,0:T(8,128)} copy(f32[3,256,512]{2,1,0:T(8,128)S(1)} %get-tuple-element.12) | data formatting | bytes 3145728
  86.8 0.7 copy.12
Async XLA Ops:
  0.6 1.4 %copy-start = (f32[3,256,512]{2,1,0:T(8,128)S(1)}, f32[3,256,512]{2,1,0:T(8,128)}, u32[]{:S(2)}) copy-start(f32[3,256,512]{2,1,0:T(8,128)} %fine_start.1) | copy-start | bytes 4718596
  2.0 1.0 %copy-start.1 = (f32[256,512]{1,0:T(8,128)S(1)}, f32[256,512]{1,0:T(8,128)}, u32[]{:S(2)}) copy-start(f32[256,512]{1,0:T(8,128)} %fine_mu.1) | copy-start | bytes 1572868
  3.1 1.0 %copy-start.2 = (f32[3,16,2048]{2,1,0:T(8,128)S(1)}, f32[3,16,2048]{2,1,0:T(8,128)}, u32[]{:S(2)}) copy-start(f32[3,16,2048]{2,1,0:T(8,128)} %coarse_start.1) | copy-start | bytes 1179652
  4.1 1.0 %copy-start.3 = (f32[3,16,2048]{2,1,0:T(8,128)S(1)}, f32[3,16,2048]{2,1,0:T(8,128)}, u32[]{:S(2)}) copy-start(f32[3,16,2048]{2,1,0:T(8,128)} %coarse_known.1) | copy-start | bytes 1179652
  5.1 0.9 %copy-start.4 = (f32[16,2048]{1,0:T(8,128)S(1)}, f32[16,2048]{1,0:T(8,128)}, u32[]{:S(2)}) copy-start(f32[16,2048]{1,0:T(8,128)} %coarse_mu.1) | copy-start | bytes 393220
where the time goes:
time: 87.8 us; the launch traced here: 87.5 us
  Pallas kernels  79 us (90%)
  local copies, waits for them, and re-layouts  7.85 us (9%)
    pallas_call x1, Pallas kernels, on_device(): pl.pallas_call(functools.partial(kernel, n_gx, n_gy, cells_total), out_sh...  79 us
    unnamed x12, local copies, waits for them, and re-layouts  7.22 us

commit v1 on v0

--- a/solution.py
+++ b/solution.py
@@ -10,6 +10,7 @@
 ITERS = 3
 LANES = 128
 SUB = 8
+UNROLL = 2
 MESH = pl.DeviceIdType.MESH
 DIRECTIONS = ((-1, 0), (1, 0), (0, -1), (0, 1), (-1, -1), (1, 1), (-1, 1), (1, -1))
 
@@ -51,14 +52,16 @@
     raw_start,
     raw_known,
     raw_mu,
-    fine,
+    fine_a,
+    fine_b,
     known,
     diag,
     inverse,
     patch_start,
     patch_known,
     patch_mu,
-    coarse,
+    coarse_a,
+    coarse_b,
     patch_out,
     row_send,
     col_send,
@@ -87,6 +90,7 @@
 ):
     gx = lax.axis_index("gx")
     gy = lax.axis_index("gy")
+    fine, coarse = (fine_a, fine_b), (coarse_a, coarse_b)
     comps, rows, width = patch_start.shape
     halves = width // LANES
     blocks = rows // SUB
@@ -217,19 +221,22 @@
         )
 
     def split_field(raw, put):
-        def body(i, carry):
-            comp, block = i // blocks, i % blocks
-            for parity in range(2):
-                for half in range(halves):
-                    at = pl.ds(block * 2 * SUB + parity, SUB, stride=2)
-                    even, odd = split_columns(
-                        raw[2 * half, comp, at, :], raw[2 * half + 1, comp, at, :]
-                    )
-                    put(comp, parity, 0, half, block, even)
-                    put(comp, parity, 1, half, block, odd)
+        def body(block, carry):
+            out = []
+            for comp in range(comps):
+                for parity in range(2):
+                    for half in range(halves):
+                        at = pl.ds(block * 2 * SUB + parity, SUB, stride=2)
+                        both = split_columns(
+                            raw[2 * half, comp, at, :], raw[2 * half + 1, comp, at, :]
+                        )
+                        out.append((comp, parity, half, both))
+            for comp, parity, half, both in out:
+                put(comp, parity, 0, half, block, both[0])
+                put(comp, parity, 1, half, block, both[1])
             return carry
 
-        lax.fori_loop(0, comps * blocks, body, 0)
+        lax.fori_loop(0, blocks, body, 0)
 
     def rows_of(block, shift=0):
         if shift == 0:
@@ -240,20 +247,23 @@
         return pl.ds(pl.multiple_of(block * SUB, SUB), SUB)
 
     def put_start(comp, parity, side, half, block, cells):
-        fine[0, comp, parity, side, half, rows_of(block), :] = cells
+        fine[0][comp, parity, side, half, rows_of(block), :] = cells
 
     def put_known(comp, parity, side, half, block, cells):
         known[comp, parity, side, half, plain(block), :] = cells
 
     def split_mu(block, carry):
+        out = []
         for parity in range(2):
             for half in range(halves):
                 at = pl.ds(block * 2 * SUB + parity, SUB, stride=2)
                 both = split_columns(raw_mu[2 * half, at, :], raw_mu[2 * half + 1, at, :])
                 for side in range(2):
                     total = both[side] + 1.0
-                    diag[parity, side, half, plain(block), :] = total
-                    inverse[parity, side, half, plain(block), :] = 1.0 / total
+                    out.append((parity, side, half, total, 1.0 / total))
+        for parity, side, half, total, reciprocal in out:
+            diag[parity, side, half, plain(block), :] = total
+            inverse[parity, side, half, plain(block), :] = reciprocal
         return carry
 
     tiles = 2 * halves
@@ -262,22 +272,22 @@
     split_field(raw_start, put_start)
     for copy in loads[tiles : 2 * tiles]:
         copy.wait()
-    lax.fori_loop(0, blocks, split_mu, 0)
+    lax.fori_loop(0, blocks, split_mu, 0, unroll=2)
     for copy in loads[2 * tiles :]:
         copy.wait()
     split_field(raw_known, put_known)
 
     wait_moves(0)
 
-    def place_start(i, carry):
-        comp, block = i // blocks, i % blocks
-        for half in range(halves):
-            coarse[0, comp, half, rows_of(block), :] = patch_start[
-                comp, plain(block), half * LANES : (half + 1) * LANES
-            ]
+    def place_start(block, carry):
+        for comp in range(comps):
+            for half in range(halves):
+                coarse[0][comp, half, rows_of(block), :] = patch_start[
+                    comp, plain(block), half * LANES : (half + 1) * LANES
+                ]
         return carry
 
-    lax.fori_loop(0, comps * blocks, place_start, 0)
+    lax.fori_loop(0, blocks, place_start, 0, unroll=4)
 
     def exchange(sweep, buf):
         for way, (parity, line) in enumerate(((0, SUB), (1, SUB + rows - 1))):
@@ -285,30 +295,10 @@
                 for comp in range(comps):
                     for side in range(2):
                         at = 2 * comp + side
-                        row_send[sweep, way, half, at : at + 1, :] = fine[
-                            buf, comp, parity, side, half, line : line + 1, :
+                        row_send[sweep, way, half, at : at + 1, :] = fine[buf][comp, parity, side, half, line : line + 1, :
                         ]
-                    row_send[sweep, way, half, SUB + comp : SUB + comp + 1, :] = coarse[
-                        buf, comp, half, line : line + 1, :
+                    row_send[sweep, way, half, SUB + comp : SUB + comp + 1, :] = coarse[buf][comp, half, line : line + 1, :
                     ]
-
-        def gather(block, carry):
-            for way, (half, at, side) in enumerate(((0, 0, 0), (halves - 1, LANES - 1, 1))):
-                cells = jnp.zeros((SUB, LANES), jnp.float32)
-                for k in range(3 * comps):
-                    if k < 2 * comps:
-                        edge = fine[buf, k // 2, k % 2, side, half, rows_of(block), :]
-                    else:
-                        edge = coarse[buf, k - 2 * comps, half, rows_of(block), :]
-                    cells = jnp.where(lane == k, roll_lanes(edge, k - at), cells)
-                col_send[way, plain(block), :] = cells
-            return carry
-
-        lax.fori_loop(0, blocks, gather, 0)
-        for way in range(2):
-            turned = col_send[way, :, :].T
-            col_turned = turned[: 2 * SUB]
-            col_out[sweep, way, :, :] = col_turned
 
         def message(direction):
             dx, dy = DIRECTIONS[direction]
@@ -331,7 +321,31 @@
                 device_id_type=MESH,
             )
 
-        for direction in range(8):
+        for direction in (4, 5, 6, 7, 0, 1):
+
+            @pl.when(inside(direction))
+            def _():
+                message(direction).start()
+
+        def gather(block, carry):
+            for way, (half, at, side) in enumerate(((0, 0, 0), (halves - 1, LANES - 1, 1))):
+                cells = jnp.zeros((SUB, LANES), jnp.float32)
+                for k in range(3 * comps):
+                    if k < 2 * comps:
+                        edge = fine[buf][k // 2, k % 2, side, half, rows_of(block), :]
+                    else:
+                        edge = coarse[buf][k - 2 * comps, half, rows_of(block), :]
+                    cells = jnp.where(lane == k, roll_lanes(edge, k - at), cells)
+                col_send[way, plain(block), :] = cells
+            return carry
+
+        lax.fori_loop(0, blocks, gather, 0, unroll=4)
+        for way in range(2):
+            turned = col_send[way, :, :].T
+            col_turned = turned[: 2 * SUB]
+            col_out[sweep, way, :, :] = col_turned
+
+        for direction in (2, 3):
 
             @pl.when(inside(direction))
             def _():
@@ -348,14 +362,14 @@
             for comp in range(comps):
                 for side in range(2):
                     at = 2 * comp + side
-                    fine[buf, comp, 1, side, half, SUB - 1 : SUB, :] = row_recv[
+                    fine[buf][comp, 1, side, half, SUB - 1 : SUB, :] = row_recv[
                         sweep, 0, half, at : at + 1, :
                     ]
-                    fine[buf, comp, 0, side, half, SUB + rows : SUB + rows + 1, :] = row_recv[
+                    fine[buf][comp, 0, side, half, SUB + rows : SUB + rows + 1, :] = row_recv[
                         sweep, 1, half, at : at + 1, :
                     ]
                 for way, line in enumerate((SUB - 1, SUB + rows)):
-                    coarse[buf, comp, half, line : line + 1, :] = row_recv[
+                    coarse[buf][comp, half, line : line + 1, :] = row_recv[
                         sweep, way, half, SUB + comp : SUB + comp + 1, :
                     ]
         left_halo[SUB : SUB + rows, :] = col_recv[sweep, 0].T
@@ -373,95 +387,108 @@
                 target[line : line + 1, :] = held[0:1, :]
 
     def halo_pair(k, lines):
-        left = pltpu.roll(left_halo[lines, :], lax.rem(LANES - k, LANES), 1)
-        right = pltpu.roll(right_halo[lines, :], lax.rem(LANES - 1 - k, LANES), 1)
+        left = roll_lanes(left_halo[lines, :], -k)
+        right = roll_lanes(right_halo[lines, :], LANES - 1 - k)
         return left, right
 
     def coarse_pass(buf, last):
-        def body(i, total):
-            comp, block = i // blocks, i % blocks
-            k = 2 * comps + comp
-            left, right = halo_pair(k, rows_of(block))
-            own = [coarse[buf, comp, half, rows_of(block), :] for half in range(halves)]
-            lefts, rights = from_left(own, left), from_right(own, right)
-            for half in range(halves):
-                columns = slice(half * LANES, (half + 1) * LANES)
-                near = (
-                    coarse[buf, comp, half, rows_of(block, 1), :]
-                    + coarse[buf, comp, half, rows_of(block, -1), :]
-                    + rights[half]
-                    + lefts[half]
-                )
-                below = (
-                    fine[buf, comp, 0, 0, half, rows_of(block), :]
-                    + fine[buf, comp, 1, 0, half, rows_of(block), :]
-                    + fine[buf, comp, 0, 1, half, rows_of(block), :]
-                    + fine[buf, comp, 1, 1, half, rows_of(block), :]
-                )
-                scale = patch_mu[plain(block), columns] + 1.0
-                res = (
-                    patch_known[comp, plain(block), columns]
-                    + 0.25 * near
-                    + 0.125 * below
-                    - scale * own[half]
-                )
-                total = total + res * res
-                new = own[half] + res / scale
+        def body(block, totals):
+            totals = list(totals)
+            lines = plain(block)
+            out = []
+            scales = [
+                patch_mu[lines, half * LANES : (half + 1) * LANES] + 1.0 for half in range(halves)
+            ]
+            reciprocals = [1.0 / scale for scale in scales]
+            for comp in range(comps):
+                left, right = halo_pair(2 * comps + comp, rows_of(block))
+                own = [coarse[buf][comp, half, rows_of(block), :] for half in range(halves)]
+                lefts, rights = from_left(own, left), from_right(own, right)
+                for half in range(halves):
+                    columns = slice(half * LANES, (half + 1) * LANES)
+                    near = (
+                        coarse[buf][comp, half, rows_of(block, 1), :]
+                        + coarse[buf][comp, half, rows_of(block, -1), :]
+                        + rights[half]
+                        + lefts[half]
+                    )
+                    below = (
+                        fine[buf][comp, 0, 0, half, rows_of(block), :]
+                        + fine[buf][comp, 1, 0, half, rows_of(block), :]
+                        + fine[buf][comp, 0, 1, half, rows_of(block), :]
+                        + fine[buf][comp, 1, 1, half, rows_of(block), :]
+                    )
+                    res = (
+                        patch_known[comp, lines, columns]
+                        + 0.25 * near
+                        + 0.125 * below
+                        - scales[half] * own[half]
+                    )
+                    totals[comp] = totals[comp] + res * res
+                    out.append((comp, half, own[half] + res * reciprocals[half]))
+            for comp, half, new in out:
                 if last:
-                    patch_out[comp, plain(block), columns] = new
+                    patch_out[comp, lines, half * LANES : (half + 1) * LANES] = new
                 else:
-                    coarse[1 - buf, comp, half, rows_of(block), :] = new
-            return total
-
-        return lax.fori_loop(0, comps * blocks, body, jnp.zeros((SUB, LANES), jnp.float32))
+                    coarse[1 - buf][comp, half, rows_of(block), :] = new
+            return tuple(totals)
+
+        zero = jnp.zeros((SUB, LANES), jnp.float32)
+        return sum(lax.fori_loop(0, blocks, body, (zero,) * comps, unroll=UNROLL))
 
     def fine_pass(buf):
-        def body(i, total):
-            comp, block = i // blocks, i % blocks
-            k = 2 * comps + comp
-            mid = [coarse[buf, comp, half, rows_of(block), :] for half in range(halves)]
-            mid_left, mid_right = halo_pair(k, rows_of(block))
-            for parity in range(2):
-                shift = 1 if parity else -1
-                far_left, far_right = halo_pair(k, rows_of(block, shift))
-                line = [
-                    0.75 * mid[half]
-                    + 0.25 * coarse[buf, comp, half, rows_of(block, shift), :]
-                    for half in range(halves)
-                ]
-                line_left = from_left(line, 0.75 * mid_left + 0.25 * far_left)
-                line_right = from_right(line, 0.75 * mid_right + 0.25 * far_right)
-                fine_left, fine_right = halo_pair(2 * comp + parity, rows_of(block))
-                evens = [fine[buf, comp, parity, 0, half, rows_of(block), :] for half in range(halves)]
-                odds = [fine[buf, comp, parity, 1, half, rows_of(block), :] for half in range(halves)]
-                before, after = from_left(odds, fine_left), from_right(evens, fine_right)
-                for half in range(halves):
-                    for side in range(2):
-                        own = odds[half] if side else evens[half]
-                        lateral = (
-                            evens[half] + after[half] if side else odds[half] + before[half]
-                        )
-                        near = (
-                            fine[buf, comp, 1 - parity, side, half, rows_of(block), :]
-                            + fine[buf, comp, 1 - parity, side, half, rows_of(block, shift), :]
-                            + lateral
-                        )
-                        spread = 0.75 * line[half] + 0.25 * (
-                            line_right[half] if side else line_left[half]
-                        )
-                        res = (
-                            known[comp, parity, side, half, plain(block), :]
-                            + 0.25 * near
-                            + 0.5 * spread
-                            - diag[parity, side, half, plain(block), :] * own
-                        )
-                        total = total + res * res
-                        fine[1 - buf, comp, parity, side, half, rows_of(block), :] = (
-                            own + res * inverse[parity, side, half, plain(block), :]
-                        )
-            return total
-
-        return lax.fori_loop(0, comps * blocks, body, jnp.zeros((SUB, LANES), jnp.float32))
+        def body(block, totals):
+            totals = list(totals)
+            out = []
+            for comp in range(comps):
+                k = 2 * comps + comp
+                mid = [coarse[buf][comp, half, rows_of(block), :] for half in range(halves)]
+                mid_left, mid_right = halo_pair(k, rows_of(block))
+                for parity in range(2):
+                    shift = 1 if parity else -1
+                    far_left, far_right = halo_pair(k, rows_of(block, shift))
+                    line = [
+                        0.75 * mid[half]
+                        + 0.25 * coarse[buf][comp, half, rows_of(block, shift), :]
+                        for half in range(halves)
+                    ]
+                    line_left = from_left(line, 0.75 * mid_left + 0.25 * far_left)
+                    line_right = from_right(line, 0.75 * mid_right + 0.25 * far_right)
+                    fine_left, fine_right = halo_pair(2 * comp + parity, rows_of(block))
+                    evens, odds = (
+                        [fine[buf][comp, parity, side, half, rows_of(block), :] for half in range(halves)]
+                        for side in range(2)
+                    )
+                    before, after = from_left(odds, fine_left), from_right(evens, fine_right)
+                    for half in range(halves):
+                        for side in range(2):
+                            own = odds[half] if side else evens[half]
+                            lateral = (
+                                evens[half] + after[half] if side else odds[half] + before[half]
+                            )
+                            near = (
+                                fine[buf][comp, 1 - parity, side, half, rows_of(block), :]
+                                + fine[buf][comp, 1 - parity, side, half, rows_of(block, shift), :]
+                                + lateral
+                            )
+                            spread = 0.75 * line[half] + 0.25 * (
+                                line_right[half] if side else line_left[half]
+                            )
+                            res = (
+                                known[comp, parity, side, half, plain(block), :]
+                                + 0.25 * near
+                                + 0.5 * spread
+                                - diag[parity, side, half, plain(block), :] * own
+                            )
+                            totals[comp] = totals[comp] + res * res
+                            new = own + res * inverse[parity, side, half, plain(block), :]
+                            out.append((comp, parity, side, half, new))
+            for comp, parity, side, half, new in out:
+                fine[1 - buf][comp, parity, side, half, rows_of(block), :] = new
+            return tuple(totals)
+
+        zero = jnp.zeros((SUB, LANES), jnp.float32)
+        return sum(lax.fori_loop(0, blocks, body, (zero,) * comps))
 
     def back_place(owner, place):
         return (
@@ -538,19 +565,21 @@
     weave_a = jnp.where(lane % 2 == 0, lane // 2, lane // 2 + LANES // 2)
     weave_b = jnp.where(lane % 2 == 0, lane // 2 + LANES // 2, lane // 2)
 
-    def weave(i, carry):
-        comp, block = i // blocks, i % blocks
-        for parity in range(2):
-            for half in range(halves):
-                even = fine[final, comp, parity, 0, half, rows_of(block), :]
-                odd = pltpu.roll(fine[final, comp, parity, 1, half, rows_of(block), :], LANES // 2, 1)
-                at = pl.ds(block * 2 * SUB + parity, SUB, stride=2)
-                raw_start[2 * half, comp, at, :] = jnp.take_along_axis(
-                    jnp.where(half_lane, even, odd), weave_a, axis=1
-                )
-                raw_start[2 * half + 1, comp, at, :] = jnp.take_along_axis(
-                    jnp.where(half_lane, odd, even), weave_b, axis=1
-                )
+    def weave(block, carry):
+        out = []
+        for comp in range(comps):
+            for parity in range(2):
+                for half in range(halves):
+                    even = fine[final][comp, parity, 0, half, rows_of(block), :]
+                    odd = fine[final][comp, parity, 1, half, rows_of(block), :]
+                    odd = pltpu.roll(odd, LANES // 2, 1)
+                    at = pl.ds(block * 2 * SUB + parity, SUB, stride=2)
+                    a = jnp.take_along_axis(jnp.where(half_lane, even, odd), weave_a, axis=1)
+                    b = jnp.take_along_axis(jnp.where(half_lane, odd, even), weave_b, axis=1)
+                    out.append((2 * half, comp, at, a))
+                    out.append((2 * half + 1, comp, at, b))
+        for tile, comp, at, cells in out:
+            raw_start[tile, comp, at, :] = cells
         return carry
 
     stores = [
@@ -563,7 +592,7 @@
     ]
 
     def put_fine():
-        lax.fori_loop(0, comps * blocks, weave, 0)
+        lax.fori_loop(0, blocks, weave, 0)
         for copy in stores:
             copy.start()
 
@@ -603,14 +632,16 @@
             pltpu.VMEM((tiles, comps, fine_rows, LANES), f32),
             pltpu.VMEM((tiles, comps, fine_rows, LANES), f32),
             pltpu.VMEM((tiles, fine_rows, LANES), f32),
-            pltpu.VMEM((2, comps, 2, 2, halves, padded, LANES), f32),
+            pltpu.VMEM((comps, 2, 2, halves, padded, LANES), f32),
+            pltpu.VMEM((comps, 2, 2, halves, padded, LANES), f32),
             pltpu.VMEM((comps, 2, 2, halves, rows, LANES), f32),
             pltpu.VMEM((2, 2, halves, rows, LANES), f32),
             pltpu.VMEM((2, 2, halves, rows, LANES), f32),
             pltpu.VMEM((comps, rows, width), f32),
             pltpu.VMEM((comps, rows, width), f32),
             pltpu.VMEM((rows, width), f32),
-            pltpu.VMEM((2, comps, halves, padded, LANES), f32),
+            pltpu.VMEM((comps, halves, padded, LANES), f32),
+            pltpu.VMEM((comps, halves, padded, LANES), f32),
             pltpu.VMEM((comps, rows, width), f32),
             pltpu.VMEM((ITERS, 2, halves, 2 * SUB, LANES), f32),
             pltpu.VMEM((2, rows, LANES), f32),

time: 87.8 us -> 65.4 us (0.74)
  Pallas kernels: 79 us -> 56.6 us
    pallas_call x1, Pallas kernels: 79 us -> 56.6 us  [on_device(): pl.pallas_call(functools.partial(kernel, n_gx, n_gy, cells_total), out_sh...]
where the time goes in v1:
time: 65.4 us; the launch traced here: 65.1 us
  Pallas kernels  56.6 us (87%)
  local copies, waits for them, and re-layouts  7.85 us (12%)
    pallas_call x1, Pallas kernels, on_device(): pl.pallas_call(functools.partial(kernel, n_gx, n_gy, cells_total), out_sh...  56.6 us
    unnamed x12, local copies, waits for them, and re-layouts  7.22 us

profile of v1, /device:TPU:0, one launch (start us, length us, event | category | flops | bytes accessed | tf_op | source)
XLA Modules:
  0.0 65.1 jit_solution(18058177163745016784)
XLA Ops:
  0.6 0.0 copy-start
  0.6 1.4 %copy-done = f32[3,256,512]{2,1,0:T(8,128)S(1)} copy-done((f32[3,256,512]{2,1,0:T(8,128)S(1)}, f32[3,256,512]{2,1,0:T(8,128)}, u32[]{:S(2)}) %copy-start) | copy-done | bytes 1572888
  2.0 0.0 copy-start.1
  2.0 1.0 %copy-done.1 = f32[256,512]{1,0:T(8,128)S(1)} copy-done((f32[256,512]{1,0:T(8,128)S(1)}, f32[256,512]{1,0:T(8,128)}, u32[]{:S(2)}) %copy-start.1) | copy-done | bytes 524312
  3.1 0.0 copy-start.2
  3.1 1.0 %copy-done.2 = f32[3,16,2048]{2,1,0:T(8,128)S(1)} copy-done((f32[3,16,2048]{2,1,0:T(8,128)S(1)}, f32[3,16,2048]{2,1,0:T(8,128)}, u32[]{:S(2)}) %copy-start.2) | copy-done | bytes 393240
  4.1 0.0 copy-start.3
  4.1 1.0 %copy-done.3 = f32[3,16,2048]{2,1,0:T(8,128)S(1)} copy-done((f32[3,16,2048]{2,1,0:T(8,128)S(1)}, f32[3,16,2048]{2,1,0:T(8,128)}, u32[]{:S(2)}) %copy-start.3) | copy-done | bytes 393240
  5.1 0.0 copy-start.4
  5.1 0.9 %copy-done.4 = f32[16,2048]{1,0:T(8,128)S(1)} copy-done((f32[16,2048]{1,0:T(8,128)S(1)}, f32[16,2048]{1,0:T(8,128)}, u32[]{:S(2)}) %copy-start.4) | copy-done | bytes 131096
  6.0 56.6 %shard_map.85 = (f32[3,256,512]{2,1,0:T(8,128)S(1)}, f32[3,16,2048]{2,1,0:T(8,128)S(1)}, f32[8,128]{1,0:T(8,128)S(1)}) custom-call(f32[3,256,512]{2,1,0:T(8,128)S(1)} %copy-done, f32[3,256,512]{2,1,0:T(8,128)} %fine_known.1, f32[256,512]{1,0:T(8,128)S(1)} %copy-done.1, f32[3,16,2048]{2,1,0:T(8,128)S(1)} %copy-done.2, f32[3,16,2048]{2,1,0:T(8,128)S(1)} %copy-done.3, ...), custom_call_target="tpu_custom_call" | custom-call | tf_op jit(solution)/shard_map/pallas_call | solution.py:622
  62.6 0.6 slice_reduce_fusion
  63.2 1.1 %copy.11 = f32[3,256,512]{2,1,0:T(8,128)} copy(f32[3,256,512]{2,1,0:T(8,128)S(1)} %get-tuple-element.12) | data formatting | bytes 3145728
  64.4 0.7 %copy.12 = f32[3,16,2048]{2,1,0:T(8,128)} copy(f32[3,16,2048]{2,1,0:T(8,128)S(1)} %get-tuple-element.13) | data formatting | bytes 786432
Async XLA Ops:
  0.6 1.4 %copy-start = (f32[3,256,512]{2,1,0:T(8,128)S(1)}, f32[3,256,512]{2,1,0:T(8,128)}, u32[]{:S(2)}) copy-start(f32[3,256,512]{2,1,0:T(8,128)} %fine_start.1) | copy-start | bytes 4718596
  2.0 1.0 %copy-start.1 = (f32[256,512]{1,0:T(8,128)S(1)}, f32[256,512]{1,0:T(8,128)}, u32[]{:S(2)}) copy-start(f32[256,512]{1,0:T(8,128)} %fine_mu.1) | copy-start | bytes 1572868
  3.1 1.0 %copy-start.2 = (f32[3,16,2048]{2,1,0:T(8,128)S(1)}, f32[3,16,2048]{2,1,0:T(8,128)}, u32[]{:S(2)}) copy-start(f32[3,16,2048]{2,1,0:T(8,128)} %coarse_start.1) | copy-start | bytes 1179652
  4.1 1.0 %copy-start.3 = (f32[3,16,2048]{2,1,0:T(8,128)S(1)}, f32[3,16,2048]{2,1,0:T(8,128)}, u32[]{:S(2)}) copy-start(f32[3,16,2048]{2,1,0:T(8,128)} %coarse_known.1) | copy-start | bytes 1179652
  5.1 0.9 %copy-start.4 = (f32[16,2048]{1,0:T(8,128)S(1)}, f32[16,2048]{1,0:T(8,128)}, u32[]{:S(2)}) copy-start(f32[16,2048]{1,0:T(8,128)} %coarse_mu.1) | copy-start | bytes 393220

commit v2 on v1

--- a/solution.py
+++ b/solution.py
@@ -63,14 +63,18 @@
     coarse_a,
     coarse_b,
     patch_out,
+    fine_row_send,
+    fine_row_recv,
+    fine_col_send,
+    fine_col_recv,
     row_send,
+    row_recv,
     col_send,
-    col_out,
-    row_recv,
     col_recv,
     corner_recv,
-    left_halo,
-    right_halo,
+    packed,
+    fine_halo,
+    coarse_halo,
     norm_x,
     norm_y,
     load_sem,
@@ -78,6 +82,8 @@
     own_sem,
     move_send,
     move_recv,
+    fine_send,
+    fine_recv,
     halo_send,
     halo_recv,
     back_own,
@@ -110,11 +116,8 @@
     for copy in loads:
         copy.start()
 
-    row_recv[...] = jnp.zeros_like(row_recv)
-    col_recv[...] = jnp.zeros_like(col_recv)
-    corner_recv[...] = jnp.zeros_like(corner_recv)
-    col_send[...] = jnp.zeros_like(col_send)
-    row_send[...] = jnp.zeros_like(row_send)
+    for ref in (fine_row_recv, fine_col_recv, row_recv, col_recv, corner_recv, row_send, fine_row_send):
+        ref[...] = jnp.zeros_like(ref)
 
     barrier = pltpu.get_barrier_semaphore()
 
@@ -199,14 +202,15 @@
 
         lax.fori_loop(1, n_gy, body, 0)
 
-    for which in range(3):
-
-        def send_step(step, carry, which=which):
+    def send_moves(which):
+        def body(step, carry):
             peer_move(which, step).start()
             return carry
 
-        lax.fori_loop(1, n_gy, send_step, 0)
+        lax.fori_loop(1, n_gy, body, 0)
         own_move(which).start()
+
+    send_moves(0)
 
     half_lane = lane < LANES // 2
     evens_first = jnp.where(half_lane, 2 * lane, 2 * lane - LANES + 1)
@@ -266,19 +270,6 @@
             inverse[parity, side, half, plain(block), :] = reciprocal
         return carry
 
-    tiles = 2 * halves
-    for copy in loads[:tiles]:
-        copy.wait()
-    split_field(raw_start, put_start)
-    for copy in loads[tiles : 2 * tiles]:
-        copy.wait()
-    lax.fori_loop(0, blocks, split_mu, 0, unroll=2)
-    for copy in loads[2 * tiles :]:
-        copy.wait()
-    split_field(raw_known, put_known)
-
-    wait_moves(0)
-
     def place_start(block, carry):
         for comp in range(comps):
             for half in range(halves):
@@ -287,109 +278,142 @@
                 ]
         return carry
 
-    lax.fori_loop(0, blocks, place_start, 0, unroll=4)
-
-    def exchange(sweep, buf):
-        for way, (parity, line) in enumerate(((0, SUB), (1, SUB + rows - 1))):
+    def pack(edges, target):
+        def body(block, carry):
+            out = []
+            for way, at in ((0, 0), (1, LANES - 1)):
+                for k, edge in enumerate(edges(way, block)):
+                    out.append((SUB * way + k, roll_lanes(edge, SUB * way + k - at)))
+            cells = jnp.zeros((SUB, LANES), jnp.float32)
+            for k, edge in out:
+                cells = jnp.where(lane == k, edge, cells)
+            packed[plain(block), :] = cells
+            return carry
+
+        lax.fori_loop(0, blocks, body, 0, unroll=4)
+        target[...] = packed[...].T[: 2 * SUB]
+
+    def message(rows_out, rows_in, cols_out, cols_in, sends, recvs, sweep, direction):
+        dx, dy = DIRECTIONS[direction]
+        way = direction % 2
+        if direction < 2:
+            source, target = rows_out.at[sweep, way], rows_in.at[sweep, 1 - way]
+        elif direction < 4:
+            source = cols_out.at[sweep, pl.ds(SUB * way, SUB), :]
+            target = cols_in.at[sweep, pl.ds(SUB * (1 - way), SUB), :]
+        else:
+            half = 0 if dy < 0 else halves - 1
+            source = rows_out.at[sweep, 0 if dx < 0 else 1, half]
+            target = corner_recv.at[sweep, (direction ^ 1) - 4]
+        return pltpu.make_async_remote_copy(
+            source,
+            target,
+            sends.at[sweep, direction],
+            recvs.at[sweep, direction ^ 1],
+            device_id={"gx": gx + dx, "gy": gy + dy},
+            device_id_type=MESH,
+        )
+
+    fine_message = functools.partial(
+        message, fine_row_send, fine_row_recv, fine_col_send, fine_col_recv, fine_send, fine_recv
+    )
+    coarse_message = functools.partial(
+        message, row_send, row_recv, col_send, col_recv, halo_send, halo_recv
+    )
+
+    def start_all(of, sweep, directions):
+        for direction in directions:
+
+            @pl.when(inside(direction))
+            def _():
+                of(sweep, direction).start()
+
+    def wait_all(of, sweep, directions):
+        for direction in directions:
+
+            @pl.when(inside(direction))
+            def _():
+                of(sweep, direction).wait_send()
+                of(sweep, direction ^ 1).wait_recv()
+
+    def send_fine(sweep):
+        buf = sweep % 2
+        for way, line in enumerate((SUB, SUB + rows - 1)):
             for half in range(halves):
                 for comp in range(comps):
                     for side in range(2):
                         at = 2 * comp + side
-                        row_send[sweep, way, half, at : at + 1, :] = fine[buf][comp, parity, side, half, line : line + 1, :
+                        fine_row_send[sweep, way, half, at : at + 1, :] = fine[buf][
+                            comp, way, side, half, line : line + 1, :
                         ]
-                    row_send[sweep, way, half, SUB + comp : SUB + comp + 1, :] = coarse[buf][comp, half, line : line + 1, :
-                    ]
-
-        def message(direction):
-            dx, dy = DIRECTIONS[direction]
-            way = direction % 2
-            if direction < 2:
-                source, target = row_send.at[sweep, way], row_recv.at[sweep, 1 - way]
-            elif direction < 4:
-                source = col_out.at[sweep, way]
-                target = col_recv.at[sweep, 1 - way, pl.ds(0, 2 * SUB), :]
-            else:
-                half = 0 if dy < 0 else halves - 1
-                source = row_send.at[sweep, 0 if dx < 0 else 1, half, pl.ds(SUB, SUB), :]
-                target = corner_recv.at[sweep, (direction ^ 1) - 4]
-            return pltpu.make_async_remote_copy(
-                source,
-                target,
-                halo_send.at[sweep, direction],
-                halo_recv.at[sweep, direction ^ 1],
-                device_id={"gx": gx + dx, "gy": gy + dy},
-                device_id_type=MESH,
-            )
-
-        for direction in (4, 5, 6, 7, 0, 1):
-
-            @pl.when(inside(direction))
-            def _():
-                message(direction).start()
-
-        def gather(block, carry):
-            for way, (half, at, side) in enumerate(((0, 0, 0), (halves - 1, LANES - 1, 1))):
-                cells = jnp.zeros((SUB, LANES), jnp.float32)
-                for k in range(3 * comps):
-                    if k < 2 * comps:
-                        edge = fine[buf][k // 2, k % 2, side, half, rows_of(block), :]
-                    else:
-                        edge = coarse[buf][k - 2 * comps, half, rows_of(block), :]
-                    cells = jnp.where(lane == k, roll_lanes(edge, k - at), cells)
-                col_send[way, plain(block), :] = cells
-            return carry
-
-        lax.fori_loop(0, blocks, gather, 0, unroll=4)
-        for way in range(2):
-            turned = col_send[way, :, :].T
-            col_turned = turned[: 2 * SUB]
-            col_out[sweep, way, :, :] = col_turned
-
-        for direction in (2, 3):
-
-            @pl.when(inside(direction))
-            def _():
-                message(direction).start()
-
-        for direction in range(8):
-
-            @pl.when(inside(direction))
-            def _():
-                message(direction).wait_send()
-                message(direction ^ 1).wait_recv()
-
+        start_all(fine_message, sweep, (0, 1))
+
+        def edges(way, block):
+            half = way * (halves - 1)
+            return [
+                fine[buf][k // 2, k % 2, way, half, rows_of(block), :] for k in range(2 * comps)
+            ]
+
+        pack(edges, fine_col_send.at[sweep])
+        start_all(fine_message, sweep, (2, 3))
+
+    def take_fine(sweep):
+        buf = sweep % 2
+        wait_all(fine_message, sweep, range(4))
         for half in range(halves):
             for comp in range(comps):
                 for side in range(2):
                     at = 2 * comp + side
-                    fine[buf][comp, 1, side, half, SUB - 1 : SUB, :] = row_recv[
+                    fine[buf][comp, 1, side, half, SUB - 1 : SUB, :] = fine_row_recv[
                         sweep, 0, half, at : at + 1, :
                     ]
-                    fine[buf][comp, 0, side, half, SUB + rows : SUB + rows + 1, :] = row_recv[
-                        sweep, 1, half, at : at + 1, :
+                    fine[buf][comp, 0, side, half, SUB + rows : SUB + rows + 1, :] = (
+                        fine_row_recv[sweep, 1, half, at : at + 1, :]
+                    )
+        fine_halo[SUB : SUB + rows, :] = fine_col_recv[sweep].T
+
+    def send_coarse(sweep):
+        buf = sweep % 2
+        for way, line in enumerate((SUB, SUB + rows - 1)):
+            for half in range(halves):
+                for comp in range(comps):
+                    row_send[sweep, way, half, comp : comp + 1, :] = coarse[buf][
+                        comp, half, line : line + 1, :
                     ]
+        start_all(coarse_message, sweep, (4, 5, 6, 7, 0, 1))
+
+        def edges(way, block):
+            half = way * (halves - 1)
+            return [coarse[buf][k, half, rows_of(block), :] for k in range(comps)]
+
+        pack(edges, col_send.at[sweep])
+        start_all(coarse_message, sweep, (2, 3))
+
+    def take_coarse(sweep):
+        buf = sweep % 2
+        wait_all(coarse_message, sweep, range(8))
+        for half in range(halves):
+            for comp in range(comps):
                 for way, line in enumerate((SUB - 1, SUB + rows)):
                     coarse[buf][comp, half, line : line + 1, :] = row_recv[
-                        sweep, way, half, SUB + comp : SUB + comp + 1, :
+                        sweep, way, half, comp : comp + 1, :
                     ]
-        left_halo[SUB : SUB + rows, :] = col_recv[sweep, 0].T
-        right_halo[SUB : SUB + rows, :] = col_recv[sweep, 1].T
-        for target, corners, at in ((left_halo, (0, 3), LANES - 1), (right_halo, (2, 1), 0)):
-            for corner, line in zip(corners, (SUB - 1, SUB + rows)):
+        coarse_halo[SUB : SUB + rows, :] = col_recv[sweep].T
+        corner_lanes = ((0, 2), (3, 1))
+        for corners, line in zip(corner_lanes, (SUB - 1, SUB + rows)):
+            held = jnp.zeros((SUB, LANES), jnp.float32)
+            for way, corner in enumerate(corners):
                 block = corner_recv[sweep, corner]
-                held = jnp.zeros((SUB, LANES), jnp.float32)
                 for comp in range(comps):
-                    k = 2 * comps + comp
-                    held = jnp.where(
-                        lane == k, roll_lanes(pltpu.roll(block, (SUB - comp) % SUB, 0)
-                                              if comp else block, k - at), held
-                    )
-                target[line : line + 1, :] = held[0:1, :]
-
-    def halo_pair(k, lines):
-        left = roll_lanes(left_halo[lines, :], -k)
-        right = roll_lanes(right_halo[lines, :], LANES - 1 - k)
-        return left, right
+                    k = SUB * way + comp
+                    lifted = pltpu.roll(block, SUB - comp, 0) if comp else block
+                    moved = roll_lanes(lifted, k - (0 if way else LANES - 1))
+                    held = jnp.where(lane == k, moved, held)
+            coarse_halo[line : line + 1, :] = held[0:1, :]
+
+    def halo_pair(halo, k, lines):
+        cells = halo[lines, :]
+        return roll_lanes(cells, -k), roll_lanes(cells, LANES - 1 - SUB - k)
 
     def coarse_pass(buf, last):
         def body(block, totals):
@@ -401,7 +425,7 @@
             ]
             reciprocals = [1.0 / scale for scale in scales]
             for comp in range(comps):
-                left, right = halo_pair(2 * comps + comp, rows_of(block))
+                left, right = halo_pair(coarse_halo, comp, rows_of(block))
                 own = [coarse[buf][comp, half, rows_of(block), :] for half in range(halves)]
                 lefts, rights = from_left(own, left), from_right(own, right)
                 for half in range(halves):
@@ -441,12 +465,11 @@
             totals = list(totals)
             out = []
             for comp in range(comps):
-                k = 2 * comps + comp
                 mid = [coarse[buf][comp, half, rows_of(block), :] for half in range(halves)]
-                mid_left, mid_right = halo_pair(k, rows_of(block))
+                mid_left, mid_right = halo_pair(coarse_halo, comp, rows_of(block))
                 for parity in range(2):
                     shift = 1 if parity else -1
-                    far_left, far_right = halo_pair(k, rows_of(block, shift))
+                    far_left, far_right = halo_pair(coarse_halo, comp, rows_of(block, shift))
                     line = [
                         0.75 * mid[half]
                         + 0.25 * coarse[buf][comp, half, rows_of(block, shift), :]
@@ -454,7 +477,7 @@
                     ]
                     line_left = from_left(line, 0.75 * mid_left + 0.25 * far_left)
                     line_right = from_right(line, 0.75 * mid_right + 0.25 * far_right)
-                    fine_left, fine_right = halo_pair(2 * comp + parity, rows_of(block))
+                    fine_left, fine_right = halo_pair(fine_halo, 2 * comp + parity, rows_of(block))
                     evens, odds = (
                         [fine[buf][comp, parity, side, half, rows_of(block), :] for half in range(halves)]
                         for side in range(2)
@@ -519,20 +542,50 @@
 
     own_back = pltpu.make_async_copy(*back_place(gy, gy), back_own.at[0])
     row = lax.broadcasted_iota(jnp.int32, (SUB, LANES), 0)
-    sums = jnp.zeros((SUB, LANES), jnp.float32)
-    for sweep in range(ITERS):
+    totals = [None] * ITERS
+    tiles = 2 * halves
+    for copy in loads[:tiles]:
+        copy.wait()
+    split_field(raw_start, put_start)
+    send_fine(0)
+    send_moves(2)
+    for copy in loads[tiles : 2 * tiles]:
+        copy.wait()
+    lax.fori_loop(0, blocks, split_mu, 0, unroll=2)
+    for copy in loads[2 * tiles :]:
+        copy.wait()
+    split_field(raw_known, put_known)
+    wait_moves(0)
+    lax.fori_loop(0, blocks, place_start, 0, unroll=4)
+    send_coarse(0)
+    send_moves(1)
+    take_fine(0)
+    take_coarse(0)
+
+    totals[0] = fine_pass(0)
+    send_fine(1)
+    wait_moves(2)
+    wait_moves(1)
+    totals[0] = totals[0] + coarse_pass(0, False)
+    for sweep in range(1, ITERS):
         buf = sweep % 2
         last = sweep == ITERS - 1
-        exchange(sweep, buf)
-        if sweep == 0:
-            wait_moves(1)
-            wait_moves(2)
-        total = coarse_pass(buf, last)
+        if sweep == 1:
+            send_coarse(1)
+        take_coarse(sweep)
+        totals[sweep] = coarse_pass(buf, last)
         if last:
             lax.fori_loop(1, n_gy, back_start, 0)
             own_back.start()
-        total = total + fine_pass(buf)
-        sums = jnp.where(row == sweep, jnp.sum(total, axis=0, keepdims=True), sums)
+        else:
+            send_coarse(sweep + 1)
+        take_fine(sweep)
+        totals[sweep] = totals[sweep] + fine_pass(buf)
+        if not last:
+            send_fine(sweep + 1)
+    sums = jnp.zeros((SUB, LANES), jnp.float32)
+    for sweep in range(ITERS):
+        sums = jnp.where(row == sweep, jnp.sum(totals[sweep], axis=0, keepdims=True), sums)
 
     def spread_sum(slots, axis, me, count, send_sems, recv_sems, between):
         def message(step, place_step):
@@ -626,7 +679,7 @@
             jax.ShapeDtypeStruct(coarse_start.shape, f32),
             jax.ShapeDtypeStruct((SUB, LANES), f32),
         ),
-        in_specs=[anywhere] * 6,
+        in_specs=[pl.BlockSpec(memory_space=pltpu.HBM)] * 6,
         out_specs=(anywhere, anywhere, pl.BlockSpec(memory_space=pltpu.VMEM)),
         scratch_shapes=[
             pltpu.VMEM((tiles, comps, fine_rows, LANES), f32),
@@ -643,12 +696,16 @@
             pltpu.VMEM((comps, halves, padded, LANES), f32),
             pltpu.VMEM((comps, halves, padded, LANES), f32),
             pltpu.VMEM((comps, rows, width), f32),
-            pltpu.VMEM((ITERS, 2, halves, 2 * SUB, LANES), f32),
-            pltpu.VMEM((2, rows, LANES), f32),
-            pltpu.VMEM((ITERS, 2, 2 * SUB, rows), f32),
-            pltpu.VMEM((ITERS, 2, halves, 2 * SUB, LANES), f32),
-            pltpu.VMEM((ITERS, 2, LANES, rows), f32),
+            pltpu.VMEM((ITERS, 2, halves, SUB, LANES), f32),
+            pltpu.VMEM((ITERS, 2, halves, SUB, LANES), f32),
+            pltpu.VMEM((ITERS, 2 * SUB, rows), f32),
+            pltpu.VMEM((ITERS, LANES, rows), f32),
+            pltpu.VMEM((ITERS, 2, halves, SUB, LANES), f32),
+            pltpu.VMEM((ITERS, 2, halves, SUB, LANES), f32),
+            pltpu.VMEM((ITERS, 2 * SUB, rows), f32),
+            pltpu.VMEM((ITERS, LANES, rows), f32),
             pltpu.VMEM((ITERS, 4, SUB, LANES), f32),
+            pltpu.VMEM((rows, LANES), f32),
             pltpu.VMEM((padded, LANES), f32),
             pltpu.VMEM((padded, LANES), f32),
             pltpu.VMEM((n_gx, SUB, LANES), f32),
@@ -658,6 +715,8 @@
             dma((3,)),
             dma((3, n_gy)),
             dma((3, n_gy)),
+            dma((ITERS, 4)),
+            dma((ITERS, 4)),
             dma((ITERS, 8)),
             dma((ITERS, 8)),
             dma((1,)),

time: 65.4 us -> 61.3 us (0.937)
  Pallas kernels: 56.6 us -> 52.5 us
    pallas_call x1, Pallas kernels: 56.6 us -> 52.5 us  [on_device(): pl.pallas_call(functools.partial(kernel, n_gx, n_gy, cells_total), out_sh...]
where the time goes in v2:
time: 61.3 us; the launch traced here: 61 us
  Pallas kernels  52.5 us (86%)
  local copies, waits for them, and re-layouts  7.85 us (13%)
  between operations  0.65 us (1%)
    pallas_call x1, Pallas kernels, on_device(): pl.pallas_call(functools.partial(kernel, n_gx, n_gy, cells_total), out_sh...  52.5 us
    unnamed x12, local copies, waits for them, and re-layouts  7.22 us

profile of v2, /device:TPU:0, one launch (start us, length us, event | category | flops | bytes accessed | tf_op | source)
XLA Modules:
  0.0 61.0 jit_solution(2743283899011555365)
XLA Ops:
  0.6 0.0 copy-start
  0.6 1.4 %copy-done = f32[3,256,512]{2,1,0:T(8,128)S(1)} copy-done((f32[3,256,512]{2,1,0:T(8,128)S(1)}, f32[3,256,512]{2,1,0:T(8,128)}, u32[]{:S(2)}) %copy-start) | copy-done | bytes 1572888
  2.0 0.0 copy-start.1
  2.0 1.0 %copy-done.1 = f32[256,512]{1,0:T(8,128)S(1)} copy-done((f32[256,512]{1,0:T(8,128)S(1)}, f32[256,512]{1,0:T(8,128)}, u32[]{:S(2)}) %copy-start.1) | copy-done | bytes 524312
  3.1 0.0 copy-start.2
  3.1 1.0 %copy-done.2 = f32[3,16,2048]{2,1,0:T(8,128)S(1)} copy-done((f32[3,16,2048]{2,1,0:T(8,128)S(1)}, f32[3,16,2048]{2,1,0:T(8,128)}, u32[]{:S(2)}) %copy-start.2) | copy-done | bytes 393240
  4.1 0.0 copy-start.3
  4.1 1.0 %copy-done.3 = f32[3,16,2048]{2,1,0:T(8,128)S(1)} copy-done((f32[3,16,2048]{2,1,0:T(8,128)S(1)}, f32[3,16,2048]{2,1,0:T(8,128)}, u32[]{:S(2)}) %copy-start.3) | copy-done | bytes 393240
  5.1 0.0 copy-start.4
  5.1 0.9 %copy-done.4 = f32[16,2048]{1,0:T(8,128)S(1)} copy-done((f32[16,2048]{1,0:T(8,128)S(1)}, f32[16,2048]{1,0:T(8,128)}, u32[]{:S(2)}) %copy-start.4) | copy-done | bytes 131096
  6.0 52.5 %shard_map.85 = (f32[3,256,512]{2,1,0:T(8,128)S(1)}, f32[3,16,2048]{2,1,0:T(8,128)S(1)}, f32[8,128]{1,0:T(8,128)S(1)}) custom-call(f32[3,256,512]{2,1,0:T(8,128)S(1)} %copy-done, f32[3,256,512]{2,1,0:T(8,128)} %fine_known.1, f32[256,512]{1,0:T(8,128)S(1)} %copy-done.1, f32[3,16,2048]{2,1,0:T(8,128)S(1)} %copy-done.2, f32[3,16,2048]{2,1,0:T(8,128)S(1)} %copy-done.3, ...), custom_call_target="tpu_custom_call" | custom-call | tf_op jit(solution)/shard_map/pallas_call | solution.py:675
  58.4 0.6 %slice_reduce_fusion = f32[3]{0:T(128)} fusion(f32[8,128]{1,0:T(8,128)S(1)} %get-tuple-element.8), kind=kLoop, calls=%fused_computation | loop fusion | bytes 24 | tf_op jit(solution)/shard_map/slice | solution.py:734
  59.1 1.1 %copy.11 = f32[3,256,512]{2,1,0:T(8,128)} copy(f32[3,256,512]{2,1,0:T(8,128)S(1)} %get-tuple-element.12) | data formatting | bytes 3145728
  60.2 0.7 %copy.12 = f32[3,16,2048]{2,1,0:T(8,128)} copy(f32[3,16,2048]{2,1,0:T(8,128)S(1)} %get-tuple-element.13) | data formatting | bytes 786432
Async XLA Ops:
  0.6 1.4 %copy-start = (f32[3,256,512]{2,1,0:T(8,128)S(1)}, f32[3,256,512]{2,1,0:T(8,128)}, u32[]{:S(2)}) copy-start(f32[3,256,512]{2,1,0:T(8,128)} %fine_start.1) | copy-start | bytes 4718596
  2.0 1.0 %copy-start.1 = (f32[256,512]{1,0:T(8,128)S(1)}, f32[256,512]{1,0:T(8,128)}, u32[]{:S(2)}) copy-start(f32[256,512]{1,0:T(8,128)} %fine_mu.1) | copy-start | bytes 1572868
  3.1 1.0 %copy-start.2 = (f32[3,16,2048]{2,1,0:T(8,128)S(1)}, f32[3,16,2048]{2,1,0:T(8,128)}, u32[]{:S(2)}) copy-start(f32[3,16,2048]{2,1,0:T(8,128)} %coarse_start.1) | copy-start | bytes 1179652
  4.1 1.0 %copy-start.3 = (f32[3,16,2048]{2,1,0:T(8,128)S(1)}, f32[3,16,2048]{2,1,0:T(8,128)}, u32[]{:S(2)}) copy-start(f32[3,16,2048]{2,1,0:T(8,128)} %coarse_known.1) | copy-start | bytes 1179652
  5.1 0.9 %copy-start.4 = (f32[16,2048]{1,0:T(8,128)S(1)}, f32[16,2048]{1,0:T(8,128)}, u32[]{:S(2)}) copy-start(f32[16,2048]{1,0:T(8,128)} %coarse_mu.1) | copy-start | bytes 393220

commit v3 on v2

--- a/solution.py
+++ b/solution.py
@@ -728,7 +728,7 @@
             dma((n_gy,)),
         ],
         compiler_params=pltpu.CompilerParams(
-            collective_id=0, has_side_effects=True, vmem_limit_bytes=48 * 1024 * 1024
+            collective_id=0, has_side_effects=True, vmem_limit_bytes=67043328
         ),
     )(fine_start, fine_known, fine_mu, coarse_start, coarse_known, coarse_mu)
     return fine_ghost, coarse_ghost, norms[:ITERS, 0]

time: 61.3 us -> 58.6 us (0.956)
  local copies, waits for them, and re-layouts: 7.85 us -> 4.77 us
    unnamed x12 -> x4, local copies, waits for them, and re-layouts: 7.22 us -> 3.47 us
    slice x1, local copies, waits for them, and re-layouts: 0.63 us -> 1.31 us  [on_device(): return (fine_ghost, coarse_ghost, norms[:ITERS, 0])]
where the time goes in v3:
time: 58.6 us; the launch traced here: 58.4 us
  Pallas kernels  53 us (90%)
  local copies, waits for them, and re-layouts  4.77 us (8%)
  between operations  0.64 us (1%)
    pallas_call x1, Pallas kernels, on_device(): pl.pallas_call(functools.partial(kernel, n_gx, n_gy, cells_total), out_sh...  53 us
    unnamed x4, local copies, waits for them, and re-layouts  3.47 us
    slice x1, local copies, waits for them, and re-layouts, on_device(): return (fine_ghost, coarse_ghost, norms[:ITERS, 0])  1.31 us

profile of v3, /device:TPU:0, one launch (start us, length us, event | category | flops | bytes accessed | tf_op | source)
XLA Modules:
  0.0 58.4 jit_solution(14779750119073099166)
XLA Ops:
  0.6 53.0 %shard_map.85 = (f32[3,256,512]{2,1,0:T(8,128)}, f32[3,16,2048]{2,1,0:T(8,128)}, f32[8,128]{1,0:T(8,128)}) custom-call(f32[3,256,512]{2,1,0:T(8,128)} %fine_start.1, f32[3,256,512]{2,1,0:T(8,128)} %fine_known.1, f32[256,512]{1,0:T(8,128)} %fine_mu.1, f32[3,16,2048]{2,1,0:T(8,128)} %coarse_start.1, f32[3,16,2048]{2,1,0:T(8,128)} %coarse_known.1, ...), custom_call_target="tpu_custom_call" | custom-call | tf_op jit(solution)/shard_map/pallas_call | solution.py:675
  53.6 1.3 %slice_reduce_fusion = f32[3]{0:T(128)} fusion(f32[8,128]{1,0:T(8,128)} %get-tuple-element.8), kind=kLoop, calls=%fused_computation | loop fusion | bytes 24 | tf_op jit(solution)/shard_map/slice | solution.py:734
  54.9 0.0 copy-start
  54.9 2.7 %copy.11 = f32[3,256,512]{2,1,0:T(8,128)} copy(f32[3,256,512]{2,1,0:T(8,128)} %get-tuple-element.12) | data formatting | bytes 3145728
  57.7 0.0 copy-done
  57.7 0.7 %copy.12 = f32[3,16,2048]{2,1,0:T(8,128)} copy(f32[3,16,2048]{2,1,0:T(8,128)S(1)} %copy-done) | data formatting | bytes 786432
Async XLA Ops:
  54.9 2.7 %copy-start = (f32[3,16,2048]{2,1,0:T(8,128)S(1)}, f32[3,16,2048]{2,1,0:T(8,128)}, u32[]{:S(2)}) copy-start(f32[3,16,2048]{2,1,0:T(8,128)} %get-tuple-element.13) | copy-start | bytes 1179652
